TPU v7x, 32 devices: a whole 2x2x4 slice. The times are simulated.
32 devices in a mesh: ga: 2 (over x), col: 16 (over z, y, core).
Axes of the slice: x: 2, y: 2, z: 4, core: 2. Of those that a mesh axis runs over, the one named last changes fastest.
Arguments:
- queries: bfloat16 [256, 32, 128], P(('ga', 'col')), parts along dimension 0, may hold values from -6 to 6
- patches: bfloat16 [64, 16, 64, 128], P(('ga', 'col')), parts along dimension 0, may hold values from -0.5 to 0.5
- top_ids: int32 [256, 32], P(('ga', 'col')), parts along dimension 0, may hold values from 0 to 31, all different within a row
Outputs:
- scores: float32 [256, 32], P('ga', 'col'), parts along dimension 0
- top_scores: float32 [256, 32], P(('ga', 'col')), parts along dimension 0
There are 2 independent parts, one for each index of `ga`. A program takes and returns all parts, laid end to end along the dimension named above; each array names one. Nothing has to cross between parts.
Inputs may be any that keep to these rules, and one draw needn't show every extreme that they name: `top_ids`: each row names 32 different clips.
All inputs are finite; a program needn't handle non-finite values.
Results may differ from a plain program's by a relative error of at most 0.0003.
Values may be sent and summed in bfloat16 or wider, within the bound.
A program may use at most 64 MiB of HBM per device.

v0:
```python
import functools

import jax
import jax.numpy as jnp
from jax import lax
from jax.experimental import pallas as pl
from jax.experimental.pallas import tpu as pltpu
from jax.sharding import PartitionSpec as P

MESH = pl.DeviceIdType.MESH
LANES = 128
FAR = 3


def kernel(
    nz, ny, tokens, clips, rows,
    q_hbm, p_hbm, ids_hbm, scores_ref, top_ref,
    qall, pv, idv, best, got, side, mine,
    in_sem, patch_sem, z_send, far_send, y_send, recv, back_send, back_recv, side_send, side_recv, known,
):
    chips = nz * ny
    me = lax.axis_index("col")
    core = lax.rem(me, 2)
    chip = lax.div(me, 2)
    y = lax.rem(chip, ny)
    z = lax.div(chip, ny)
    partner = me + 1 - 2 * core
    _, halves, half, depth = qall.shape
    width = halves * half
    count = width // tokens
    per_clip = pv.shape[1] // clips

    def slot_of(zz, yy):
        return zz * ny + yy

    def device(slot):
        return {"col": slot * 2 + core}

    def inside(zz):
        return (zz >= 0) & (zz < nz)

    own_q = pltpu.make_async_copy(q_hbm, qall.at[chip], in_sem.at[0])
    own_q.start()
    own_p = pltpu.make_async_copy(p_hbm, pv.at[0], in_sem.at[1])
    own_p.start()
    own_i = pltpu.make_async_copy(ids_hbm, idv, in_sem.at[2])
    own_i.start()

    barrier = pltpu.get_barrier_semaphore()
    pl.semaphore_signal(barrier, inc=1, device_id={"col": partner}, device_id_type=MESH)
    greeted = 1
    if ny == 2:
        pl.semaphore_signal(barrier, inc=1, device_id=device(slot_of(z, 1 - y)), device_id_type=MESH)
        greeted = 2
    for step in (1, -1):
        there = inside(z + step)

        @pl.when(there)
        def _():
            pl.semaphore_signal(barrier, inc=1, device_id=device(slot_of(z + step, y)), device_id_type=MESH)

        greeted = greeted + jnp.where(there, 1, 0)
    pl.semaphore_wait(barrier, greeted)

    def piece(slot, h, target, sem):
        return pltpu.make_async_remote_copy(
            src_ref=qall.at[slot, h], dst_ref=qall.at[slot, h], send_sem=sem, recv_sem=recv.at[slot, h],
            device_id=target, device_id_type=MESH,
        )

    def z_copy(slot, h, way):
        return piece(slot, h, device(slot_of(z + way, y)), z_send.at[(1 - way) // 2, slot, h])

    def far_copy(row, h, way):
        slot = slot_of(z, y if row == 0 else 1 - y)
        return piece(slot, h, device(slot_of(z + FAR * way, y)), far_send.at[row, (1 - way) // 2, h])

    def y_copy(slot, h):
        return piece(slot, h, device(slot_of(z, 1 - y)), y_send.at[slot, h])

    def back_copy(slot, origin, target):
        return pltpu.make_async_remote_copy(
            src_ref=best.at[slot], dst_ref=got.at[origin], send_sem=back_send.at[slot], recv_sem=back_recv.at[origin],
            device_id=target, device_id_type=MESH,
        )

    def side_copy(slot):
        return pltpu.make_async_remote_copy(
            src_ref=best.at[slot], dst_ref=side.at[slot], send_sem=side_send.at[slot], recv_sem=side_recv.at[slot],
            device_id={"col": partner}, device_id_type=MESH,
        )

    patch_copy = pltpu.make_async_remote_copy(
        src_ref=pv.at[0], dst_ref=pv.at[1], send_sem=patch_sem.at[0], recv_sem=patch_sem.at[1],
        device_id={"col": partner}, device_id_type=MESH,
    )

    def arrived(slot, h):
        piece(slot, h, {"col": partner}, y_send.at[slot, h]).wait_recv()

    def compute(slot, sides=(0, 1)):
        q = qall[slot].reshape(width, depth)
        for i in sides:
            for j in range(clips):
                top = None
                for r in range(per_clip // rows):
                    sim = lax.dot_general(
                        pv[i, pl.ds(j * per_clip + r * rows, rows), :], q, (((1,), (1,)), ((), ())),
                        preferred_element_type=jnp.float32,
                    )
                    part = jnp.max(sim.reshape(rows // 8, 8, width), axis=0)
                    top = part if top is None else jnp.maximum(top, part)
                best[slot, pl.ds(i * clips + j, 1), :] = jnp.max(top, axis=0, keepdims=True)

    def done(slot):
        back_copy(slot, chip, device(slot)).start()
        side_copy(slot).start()

    own_q.wait()
    for h in range(halves):
        for way in (1, -1):

            @pl.when(inside(z + way))
            def _():
                z_copy(chip, h, way).start()

        if ny == 2:
            y_copy(chip, h).start()
    own_p.wait()
    patch_copy.start()
    for stage in range(1, FAR):
        for way in (1, -1):

            @pl.when(inside(z + way) & inside(z - way * stage))
            def _():
                pl.semaphore_signal(
                    known.at[(1 - way) // 2, stage - 1], inc=1,
                    device_id=device(slot_of(z + way, y)), device_id_type=MESH,
                )

        for way in (1, -1):

            @pl.when(inside(z - way * (stage + 1)))
            def _():
                pl.semaphore_wait(known.at[(1 - way) // 2, stage - 1], 1)

    for h in range(halves):
        for way in (1, -1):

            @pl.when(inside(z + FAR * way))
            def _():
                far_copy(0, h, way).start()

    compute(chip, (0,))

    def onward(z_from, d, way):
        return inside(z_from) & inside(z + way) & (d + 1 != FAR)

    def step(d, carry):
        for way in (1, -1):
            z_from = z - way * d
            slot = slot_of(z_from, y)

            @pl.when(inside(z_from))
            def _():
                for h in range(halves):
                    arrived(slot, h)

                    @pl.when(onward(z_from, d, way))
                    def _():
                        z_copy(slot, h, way).start()

                    if ny == 2:

                        @pl.when(d != FAR)
                        def _():
                            y_copy(slot, h).start()

        @pl.when(d == 1)
        def _():
            if ny == 2:
                for h in range(halves):
                    arrived(slot_of(z, 1 - y), h)
                    for way in (1, -1):

                        @pl.when(inside(z + FAR * way))
                        def _():
                            far_copy(1, h, way).start()

            patch_copy.wait_recv()
            compute(chip, (1,))
            side_copy(chip).start()

        for way in (1, -1):
            z_from = z - way * d
            slot = slot_of(z_from, y)

            @pl.when(inside(z_from) & (d < nz))
            def _():
                compute(slot)
                done(slot)

        if ny == 2:
            late(d - 1)
        return carry

    def late(d):
        for way in (1, -1):
            z_from = z - way * d
            slot = slot_of(z_from, 1 - y)

            @pl.when(inside(z_from) & ((d > 0) | (way > 0)))
            def _():
                @pl.when(d > 0)
                def _():
                    for h in range(halves):
                        arrived(slot, h)

                compute(slot)
                done(slot)

    lax.fori_loop(1, nz + (ny - 1), step, 0)

    total = 2 * chips * count
    token = lax.broadcasted_iota(jnp.int32, (width, total), 0)
    lane = lax.broadcasted_iota(jnp.int32, (width, total), 1)
    pick = jnp.where(lax.div(token, tokens) == lax.rem(lane, count), 1.0, 0.0).astype(jnp.float32)
    row_of = lax.broadcasted_iota(jnp.int32, (chips, total), 0)
    lane_of = lax.div(lax.broadcasted_iota(jnp.int32, (chips, total), 1), count)
    here = row_of == lax.div(lane_of, 2)
    ours = lax.rem(lane_of, 2) == core

    def take(i, carry):
        side_copy(i).wait_recv()
        return carry

    lax.fori_loop(0, chips, take, 0)
    for j in range(clips):
        near = jnp.dot(best[:, j, :], pick, precision=lax.Precision.HIGHEST, preferred_element_type=jnp.float32)
        far = jnp.dot(side[:, clips + j, :], pick, precision=lax.Precision.HIGHEST, preferred_element_type=jnp.float32)
        kept_sums = jnp.where(here, jnp.where(ours, near, far), 0.0)
        scores_ref[pl.ds(j, 1), :] = jnp.sum(kept_sums, axis=0, keepdims=True) / tokens

    own_i.wait()
    mine[...] = jnp.zeros_like(mine)
    got[chip] = best[chip]
    ids = idv[...]
    both = 2 * clips
    swapped = lax.rem(lax.rem(lax.div(ids, clips), 2) + core, 2)
    place = (swapped * clips + lax.rem(ids, clips)) * chips + lax.div(ids, both)
    kept = ids.shape[1]
    padded = jnp.concatenate([place, jnp.zeros((count, LANES - kept), jnp.int32)], axis=1)
    q_of = lax.broadcasted_iota(jnp.int32, (count, width), 0)
    t_of = lax.broadcasted_iota(jnp.int32, (count, width), 1)
    select = jnp.where(lax.div(t_of, tokens) == q_of, 1.0, 0.0).astype(jnp.float32)

    def collect(i, carry):
        origin = lax.rem(chip + i, chips)
        back_copy(origin, origin, {"col": partner}).wait_recv()
        return carry

    lax.fori_loop(1, chips, collect, 0)
    for j in range(both):
        mine[:, pl.ds(j * chips, chips)] = lax.dot_general(
            select, got[:, j, :], (((1,), (1,)), ((), ())),
            precision=lax.Precision.HIGHEST, preferred_element_type=jnp.float32,
        ) / tokens
    chosen = jnp.zeros((count, LANES), jnp.float32)
    for w in range(mine.shape[1] // LANES):
        local = jnp.take_along_axis(mine[:, pl.ds(w * LANES, LANES)], lax.rem(padded, LANES), axis=1)
        chosen = jnp.where(lax.div(padded, LANES) == w, local, chosen)
    top_ref[...] = chosen[:, :kept]

    patch_copy.wait_send()
    for h in range(halves):
        for way in (1, -1):

            @pl.when(inside(z + FAR * way))
            def _():
                for row in range(ny):
                    far_copy(row, h, way).wait_send()

    def left(d, carry):
        for way in (1, -1):
            z_from = z - way * d
            slot = slot_of(z_from, y)
            for h in range(halves):

                @pl.when(onward(z_from, d, way))
                def _():
                    z_copy(slot, h, way).wait_send()

                if ny == 2:

                    @pl.when(inside(z_from) & ((d > 0) | (way > 0)) & (d != FAR))
                    def _():
                        y_copy(slot, h).wait_send()

        return carry

    lax.fori_loop(0, nz, left, 0)

    def left_back(i, carry):
        slot = lax.rem(chip + i, chips)

        @pl.when(i > 0)
        def _():
            back_copy(slot, chip, device(slot)).wait_send()

        side_copy(slot).wait_send()
        return carry

    lax.fori_loop(0, chips, left_back, 0)


def across_y(mesh):
    line = mesh.devices[0]
    if len(line) % 4 or not hasattr(line[0], "coords"):
        return 1
    return 2 if len({d.coords[1] for d in line}) == 2 else 1


def solution(mesh):
    n = mesh.shape["col"]
    ny = across_y(mesh)
    nz = n // (2 * ny)

    def per_device(queries, patches, top_ids):
        clips, frames, per_frame, depth = patches.shape
        count, tokens, _ = queries.shape
        width = count * tokens
        per_clip = frames * per_frame
        kept = top_ids.shape[1]
        rows = 256
        halves = 1
        chips = nz * ny
        wide = -(-(clips * n) // LANES) * LANES
        anywhere = pl.BlockSpec(memory_space=pl.ANY)
        vmem = pl.BlockSpec(memory_space=pltpu.VMEM)
        scores, top = pl.pallas_call(
            functools.partial(kernel, nz, ny, tokens, clips, rows),
            out_shape=(
                jax.ShapeDtypeStruct((clips, n * count), jnp.float32),
                jax.ShapeDtypeStruct((count, kept), jnp.float32),
            ),
            in_specs=[anywhere] * 3,
            out_specs=(vmem, vmem),
            scratch_shapes=[
                pltpu.VMEM((chips, halves, width // halves, depth), jnp.bfloat16),
                pltpu.VMEM((2, clips * per_clip, depth), jnp.bfloat16),
                pltpu.VMEM((count, kept), jnp.int32),
                pltpu.VMEM((chips, 2 * clips, width), jnp.float32),
                pltpu.VMEM((chips, 2 * clips, width), jnp.float32),
                pltpu.VMEM((chips, 2 * clips, width), jnp.float32),
                pltpu.VMEM((count, wide), jnp.float32),
                pltpu.SemaphoreType.DMA((3,)),
                pltpu.SemaphoreType.DMA((2,)),
                pltpu.SemaphoreType.DMA((2, chips, halves)),
                pltpu.SemaphoreType.DMA((ny, 2, halves)),
                pltpu.SemaphoreType.DMA((chips, halves)),
                pltpu.SemaphoreType.DMA((chips, halves)),
                pltpu.SemaphoreType.DMA((chips,)),
                pltpu.SemaphoreType.DMA((chips,)),
                pltpu.SemaphoreType.DMA((chips,)),
                pltpu.SemaphoreType.DMA((chips,)),
                pltpu.SemaphoreType.REGULAR((2, FAR - 1)),
            ],
            compiler_params=pltpu.CompilerParams(collective_id=0, has_side_effects=True),
        )(
            queries.reshape(halves, width // halves, depth),
            patches.reshape(clips * per_clip, depth),
            top_ids,
        )
        return scores.T, top

    return jax.shard_map(
        per_device,
        mesh=mesh,
        in_specs=(
            P(("ga", "col"), None, None),
            P(("ga", "col"), None, None, None),
            P(("ga", "col"), None),
        ),
        out_specs=(P("ga", "col"), P(("ga", "col"), None)),
        check_vma=False,
    )
```

profile of v0, /device:TPU:0, one launch (start us, length us, event | category | flops | bytes accessed | tf_op | source)
XLA Modules:
  0.0 24.7 jit_solution(4425500270005265852)
XLA Ops:
  0.6 22.2 %shard_map.50 = (f32[2,128]{1,0:T(2,128)}, f32[8,32]{1,0:T(8,128)}) custom-call(bf16[1,256,128]{2,1,0:T(8,128)(2,1)} %bitcast.4, bf16[2048,128]{1,0:T(8,128)(2,1)} %bitcast.3, s32[8,32]{1,0:T(8,128)} %ids_hbm.1), custom_call_target="tpu_custom_call" | custom-call | tf_op jit(solution)/shard_map/pallas_call | solution.py:340
  22.9 0.0 copy-start
  22.9 0.0 copy-start.1
  22.9 0.6 %copy-done.1 = f32[2,128]{1,0:T(2,128)S(1)} copy-done((f32[2,128]{1,0:T(2,128)S(1)}, f32[2,128]{1,0:T(2,128)}, u32[]{:S(2)}) %copy-start.1) | copy-done | bytes 1048
  23.5 0.6 %copy.7 = f32[128,2]{0,1:T(2,128)} copy(f32[128,2]{0,1:T(2,128)S(1)} %bitcast.5) | data formatting | bytes 2048
  24.1 0.0 copy-done
  24.1 0.6 %copy.8 = f32[8,32]{1,0:T(8,128)} copy(f32[8,32]{1,0:T(8,128)S(1)} %copy-done) | data formatting | bytes 2048
Async XLA Ops:
  22.9 1.2 %copy-start = (f32[8,32]{1,0:T(8,128)S(1)}, f32[8,32]{1,0:T(8,128)}, u32[]{:S(2)}) copy-start(f32[8,32]{1,0:T(8,128)} %get-tuple-element.9) | copy-start | bytes 3076
  22.9 0.6 %copy-start.1 = (f32[2,128]{1,0:T(2,128)S(1)}, f32[2,128]{1,0:T(2,128)}, u32[]{:S(2)}) copy-start(f32[2,128]{1,0:T(2,128)} %get-tuple-element.4) | copy-start | bytes 3076
where the time goes:
time: 24.8 us; the launch traced here: 24.7 us
  Pallas kernels  22.2 us (90%)
  local copies, waits for them, and re-layouts  1.79 us (7%)
  between operations  0.66 us (3%)
    pallas_call x1, Pallas kernels, per_device(): pl.pallas_call(functools.partial(kernel, nz, ny, tokens, clips, rows), ou...  22.2 us
    unnamed x6, local copies, waits for them, and re-layouts  1.79 us

commit v1 on v0

--- a/solution.py
+++ b/solution.py
@@ -340,8 +340,8 @@
         scores, top = pl.pallas_call(
             functools.partial(kernel, nz, ny, tokens, clips, rows),
             out_shape=(
-                jax.ShapeDtypeStruct((clips, n * count), jnp.float32),
-                jax.ShapeDtypeStruct((count, kept), jnp.float32),
+                pltpu.VMEM((clips, n * count), jnp.float32),
+                pltpu.VMEM((count, kept), jnp.float32),
             ),
             in_specs=[anywhere] * 3,
             out_specs=(vmem, vmem),
@@ -371,6 +371,24 @@
             patches.reshape(clips * per_clip, depth),
             top_ids,
         )
+        def out_kernel(a, b, c, d, sem):
+            x = pltpu.make_async_copy(a, c, sem.at[0])
+            y = pltpu.make_async_copy(b, d, sem.at[1])
+            x.start()
+            y.start()
+            x.wait()
+            y.wait()
+
+        scores, top = pl.pallas_call(
+            out_kernel,
+            out_shape=(
+                jax.ShapeDtypeStruct((clips, n * count), jnp.float32),
+                jax.ShapeDtypeStruct((count, kept), jnp.float32),
+            ),
+            in_specs=[vmem, vmem],
+            out_specs=(anywhere, anywhere),
+            scratch_shapes=[pltpu.SemaphoreType.DMA((2,))],
+        )(pltpu.with_memory_space_constraint(scores, pltpu.VMEM), pltpu.with_memory_space_constraint(top, pltpu.VMEM))
         return scores.T, top
 
     return jax.shard_map(

time: 24.8 us -> 23 us (0.927)
  local copies, waits for them, and re-layouts: 1.79 us -> 0 us
    unnamed x6 -> x0, local copies, waits for them, and re-layouts: 1.79 us -> none
    pallas_call x0 -> x1, Pallas kernels: none -> 0.62 us  [per_device(): pl.pallas_call(out_kernel, out_shape=(jax.ShapeDtypeStruct((clips, n * co...]
    pallas_call x1, Pallas kernels: 22.2 us -> 21.6 us  [per_device(): pl.pallas_call(functools.partial(kernel, nz, ny, tokens, clips, rows), ou...]
where the time goes in v1:
time: 23 us; the launch traced here: 22.9 us
  Pallas kernels  22.2 us (97%)
  between operations  0.64 us (3%)
    pallas_call x1, Pallas kernels, per_device(): pl.pallas_call(functools.partial(kernel, nz, ny, tokens, clips, rows), ou...  21.6 us
    pallas_call x1, Pallas kernels, per_device(): pl.pallas_call(out_kernel, out_shape=(jax.ShapeDtypeStruct((clips, n * co...  0.62 us

profile of v1, /device:TPU:0, one launch (start us, length us, event | category | flops | bytes accessed | tf_op | source)
XLA Modules:
  0.0 22.9 jit_solution(12808705940243617466)
XLA Ops:
  0.6 21.6 %shard_map.50 = (f32[2,128]{1,0:T(2,128)S(1)}, f32[8,32]{1,0:T(8,128)S(1)}) custom-call(bf16[1,256,128]{2,1,0:T(8,128)(2,1)} %bitcast.4, bf16[2048,128]{1,0:T(8,128)(2,1)} %bitcast.3, s32[8,32]{1,0:T(8,128)} %ids_hbm.1), custom_call_target="tpu_custom_call" | custom-call | tf_op jit(solution)/shard_map/pallas_call | solution.py:340
  22.3 0.6 %shard_map.51 = (f32[2,128]{1,0:T(2,128)}, f32[8,32]{1,0:T(8,128)}) custom-call(f32[2,128]{1,0:T(2,128)S(1)} %get-tuple-element.6.a, f32[8,32]{1,0:T(8,128)S(1)} %get-tuple-element.7.b), custom_call_target="tpu_custom_call" | custom-call | tf_op jit(solution)/shard_map/pallas_call | solution.py:382
